TPU v7x, 32 devices: a whole 2x2x4 slice. The times are simulated.
32 devices in a mesh: grp: 4 (over z), seq: 8 (over y, x, core).
Axes of the slice: x: 2, y: 2, z: 4, core: 2. Of those that a mesh axis runs over, the one named last changes fastest.
Arguments:
- hist_keys: bfloat16 [4, 1024, 1024], P('grp', 'seq'), may hold values from -4 to 4
- hist_values: bfloat16 [4, 1024, 1024], P('grp', 'seq'), may hold values from -6 to 6
- latent_queries: bfloat16 [4, 64, 1024], P('grp', 'seq'), may hold values from -48 to 48
- latent_pos: int32 [4, 64], P('grp'), may hold values from 128 to 1023
- targets: int32 [4, 64], P('grp', 'seq'), may hold values from 0 to 127
- out_proj: bfloat16 [1024, 2048], P('seq'), may hold values from -0.1875 to 0.1875
- norm_gain: float32 [2048], replicated, may hold values from 0.1 to 1.9
- unembed: bfloat16 [2048, 128], replicated, may hold values from -0.125 to 0.125
Outputs:
- loss: float32 [4], P('grp')
- grad_queries: bfloat16 [4, 64, 1024], P('grp', 'seq')
- grad_keys: bfloat16 [4, 1024, 1024], P('grp', 'seq')
- grad_values: bfloat16 [4, 1024, 1024], P('grp', 'seq')
- proj_update: float32 [1024, 2048], P('seq')
All inputs are finite; a program needn't handle non-finite values.
Results may differ from a plain program's by a relative error of at most 0.03.
Values may be sent and summed in bfloat16 or wider, within the bound.
No kernel may reach another device: no remote copies, remote signals or barrier semaphores. Data moves between devices by JAX's collectives and lax.ppermute only.
A program may use at most 64 MiB of HBM per device.

v0:
```python
import jax
import jax.numpy as jnp
from jax import lax
from jax.sharding import PartitionSpec as P

D = 2048
HD = 128
epsilon = 1e-06
loss_factor = 64.0


def joined(part, axis, combine):
    gathered = jax.tree.map(lambda a: lax.all_gather(a, axis), part)

    def take(source):
        return jax.tree.map(lambda a: lax.dynamic_index_in_dim(a, source, 0, False), gathered)

    return lax.fori_loop(
        1, lax.axis_size(axis), lambda source, state: combine(state, take(source)), take(0)
    )


def repeat_heads(stat):
    return jnp.repeat(stat, HD, axis=-1)


def combine(earlier, later):
    best = jnp.maximum(earlier[0], later[0])
    factor_one = jnp.exp(earlier[0] - best)
    factor_two = jnp.exp(later[0] - best)
    denom = earlier[1] * factor_one + later[1] * factor_two
    summed = earlier[2] * repeat_heads(factor_one) + later[2] * repeat_heads(factor_two)
    return (best, denom, summed)


def body(hist_keys, hist_values, latent_queries, latent_pos, targets, out_proj, norm_gain, unembed):
    softmax_scale = HD ** (-0.5)
    seq_keys = hist_keys[0]
    seq_values = hist_values[0]
    position = lax.axis_index("seq")
    tok_rows = seq_keys.shape[0]
    channels = seq_keys.shape[1]
    head_count = channels // HD
    own_rows = latent_queries.shape[1]
    queries = lax.all_gather(latent_queries[0], "seq", axis=0, tiled=True)
    latents = queries.shape[0]
    query_heads = queries.reshape(latents, head_count, HD)
    key_heads = seq_keys.reshape(tok_rows, head_count, HD)
    value_heads = seq_values.reshape(tok_rows, head_count, HD)
    places = position * tok_rows + jnp.arange(tok_rows, dtype=jnp.int32)
    visible = (places[None, :] <= latent_pos[0][:, None])[None]
    scores = (
        jnp.einsum("ihd,jhd->hij", query_heads, key_heads, preferred_element_type=jnp.float32)
        * softmax_scale
    )
    largest = jnp.max(jnp.where(visible, scores, -1e30), axis=-1)
    weights = jnp.where(visible, jnp.exp(scores - largest[..., None]), 0.0)
    summed = jnp.sum(weights, axis=-1)
    partial_out = jnp.einsum(
        "hij,jhd->ihd",
        weights.astype(jnp.bfloat16),
        value_heads,
        preferred_element_type=jnp.float32,
    ).reshape(latents, channels)
    best, denom, combined = joined((largest.T, summed.T, partial_out), "seq", combine)
    attn_all = (combined / repeat_heads(denom)).astype(jnp.bfloat16)
    log_norm = best + jnp.log(denom)
    slab = out_proj.shape[0]
    attn_cols = lax.dynamic_slice_in_dim(attn_all, position * slab, slab, 1)
    proj_columns = lax.all_to_all(out_proj, "seq", split_axis=1, concat_axis=0, tiled=True)
    column_block = jnp.dot(attn_all, proj_columns, preferred_element_type=jnp.float32)
    hidden = lax.all_to_all(column_block, "seq", split_axis=0, concat_axis=1, tiled=True)
    inverse = lax.rsqrt(jnp.mean(hidden * hidden, axis=-1, keepdims=True) + epsilon)
    normed = (hidden * inverse * norm_gain).astype(jnp.bfloat16)
    logits = jnp.dot(normed, unembed, preferred_element_type=jnp.float32)
    log_total = jax.nn.logsumexp(logits, axis=-1, keepdims=True)
    onehot = (jnp.arange(logits.shape[1], dtype=jnp.int32)[None, :] == targets[0][:, None]).astype(
        jnp.float32
    )
    local_loss = jnp.sum(log_total[:, 0] - jnp.sum(logits * onehot, axis=-1))
    grad_logits = (loss_factor * (jnp.exp(logits - log_total) - onehot)).astype(jnp.bfloat16)
    grad_normed = lax.dot_general(
        grad_logits, unembed, (((1,), (1,)), ((), ())), preferred_element_type=jnp.float32
    )
    scaled = norm_gain * grad_normed
    grad_hidden = (
        inverse * scaled - hidden * inverse**3 * jnp.mean(hidden * scaled, axis=-1, keepdims=True)
    ).astype(jnp.bfloat16)
    grad_all = lax.all_gather(grad_hidden, "seq", axis=0, tiled=True)
    weight_part = lax.dot_general(
        attn_cols, grad_all, (((0,), (0,)), ((), ())), preferred_element_type=jnp.float32
    )
    grad_cols = lax.dot_general(
        grad_all, out_proj, (((1,), (1,)), ((), ())), preferred_element_type=jnp.float32
    ).astype(jnp.bfloat16)
    grad_attn = lax.all_gather(grad_cols, "seq", axis=1, tiled=True)
    grad_heads = grad_attn.reshape(latents, head_count, HD)
    product = grad_attn.astype(jnp.float32) * attn_all.astype(jnp.float32)
    delta = jnp.sum(product.reshape(latents, head_count, HD), axis=-1)
    probs = jnp.where(visible, jnp.exp(scores - log_norm.T[..., None]), 0.0)
    grad_probs = jnp.einsum(
        "ihd,jhd->hij", grad_heads, value_heads, preferred_element_type=jnp.float32
    )
    grad_scores = (probs * (grad_probs - delta.T[..., None])).astype(jnp.bfloat16)
    grad_values = (
        jnp.einsum(
            "hij,ihd->jhd",
            probs.astype(jnp.bfloat16),
            grad_heads,
            preferred_element_type=jnp.float32,
        )
        .reshape(tok_rows, channels)
        .astype(jnp.bfloat16)
    )
    grad_keys = (
        (
            jnp.einsum("hij,ihd->jhd", grad_scores, query_heads, preferred_element_type=jnp.float32)
            * softmax_scale
        )
        .reshape(tok_rows, channels)
        .astype(jnp.bfloat16)
    )
    terms = jnp.einsum("hij,jhd->ihd", grad_scores, key_heads, preferred_element_type=jnp.float32)
    grad_queries = lax.psum_scatter(
        (terms.reshape(lax.axis_size("seq") * own_rows, channels) * softmax_scale).astype(
            jnp.bfloat16
        ),
        "seq",
        scatter_dimension=0,
        tiled=True,
    )
    entries = channels * D
    weight_sum = lax.psum(weight_part.astype(jnp.bfloat16), "grp").astype(jnp.float32)
    loss_sum, square_sum = lax.psum((local_loss, jnp.sum(weight_sum * weight_sum)), "seq")
    proj_update = weight_sum * lax.rsqrt(square_sum / entries + epsilon)
    return (
        loss_sum.reshape(1),
        grad_queries[None],
        grad_keys[None],
        grad_values[None],
        proj_update,
    )


def solution(mesh):
    placed = (
        P("grp", "seq", None),
        P("grp", "seq", None),
        P("grp", "seq", None),
        P("grp", None),
        P("grp", "seq"),
        P("seq", None),
        P(),
        P(),
    )
    return jax.shard_map(
        body,
        mesh=mesh,
        in_specs=placed,
        out_specs=(
            P("grp"),
            P("grp", "seq", None),
            P("grp", "seq", None),
            P("grp", "seq", None),
            P("seq", None),
        ),
        check_vma=False,
    )
```

profile of v0, /device:TPU:0, one launch (start us, length us, event | category | flops | bytes accessed | tf_op | source)
XLA Modules:
  0.0 178.7 jit_solution(14543328704458842982)
XLA Ops:
  7.2 11.0 %all-gather = bf16[1,64,1024]{2,1,0:T(8,128)(2,1)S(1)} all-gather(bf16[1,8,1024]{2,1,0:T(8,128)(2,1)} %param.12), channel_id=2, replica_groups=mesh['grp'=4,'seq'=8] {'seq'}, dimensions={1}, use_global_device_ids=true | all-gather | bytes 147456 | tf_op jit(solution)/shard_map/all_gather | solution.py:45
  18.3 1.0 copy.64
  19.3 1.0 copy.65
  20.3 0.7 broadcast_compare_fusion
  21.1 0.4 select_reduce_fusion
  21.4 0.3 convolution_bitcast_fusion
  21.7 0.2 copy.46
  21.9 0.7 all_gather_reshape.3
  22.6 0.8 copy.97
  23.5 3.5 %all-to-all-start = ((bf16[128,8,256]{2,0,1:T(8,128)(2,1)}), bf16[128,8,256]{2,0,1:T(8,128)(2,1)S(1)}, u32[]{:S(2)}, u32[]{:S(2)}) async-start(bf16[128,8,256]{2,0,1:T(8,128)(2,1)} %bitcast.109), calls=%async_computation | async-start | bytes 1048576 | tf_op jit(solution)/shard_map/all_to_all | solution.py:70
  27.0 0.3 fusion.15
  27.3 14.3 %all-gather.4 = f32[8,64,8]{1,2,0:T(8,128)S(1)} all-gather(f32[1,64,8]{1,2,0:T(8,128)S(1)} %bitcast.146), channel_id=4, replica_groups=mesh['grp'=4,'seq'=8] {'seq'}, dimensions={0}, use_global_device_ids=true | all-gather | bytes 18432 | tf_op jit(solution)/shard_map/all_gather | solution.py:13
  41.5 9.5 %all-gather.3 = f32[8,64,8]{1,2,0:T(8,128)S(1)} all-gather(f32[1,64,8]{1,2,0:T(8,128)S(1)} %bitcast.145), channel_id=3, replica_groups=mesh['grp'=4,'seq'=8] {'seq'}, dimensions={0}, use_global_device_ids=true | all-gather | bytes 18432 | tf_op jit(solution)/shard_map/all_gather | solution.py:13
  51.0 2.8 %all-gather.7.cloned.1.call-done = f32[8,64,1024]{2,1,0:T(8,128)} async-done(((f32[1,64,1024]{2,1,0:T(8,128)}), f32[8,64,1024]{2,1,0:T(8,128)}) %all-gather.7.cloned.1.call-update) | async-done | bytes 2097168 | tf_op jit(solution)/shard_map/all_gather | solution.py:13
  53.8 1.0 slice_bitcast_fusion
  54.7 11.5 %while.19 = (s32[]{:T(128)}, f32[64,8]{0,1:T(8,128)S(1)}, f32[64,8]{0,1:T(8,128)S(1)}, f32[64,1024]{1,0:T(8,128)S(1)}, f32[8,64,8]{1,2,0:T(8,128)S(1)}, /*index=...) while((s32[]{:T(128)}, f32[64,8]{0,1:T(8,128)S(1)}, ...), condition=%wide.region_3.4_spmd, body=%wide.region_2.3_spmd.sunk | while | flops 199685 | bytes 1863823 | solution.py:18
  54.8 0.1 copy.105
  54.9 0.1 broadcast_in_dim.92
  55.1 0.1 broadcast_in_dim.91
  55.2 1.2 fusion.60
  56.6 0.1 broadcast_in_dim.92
  56.7 0.1 broadcast_in_dim.91
  56.9 1.2 fusion.60
  58.2 0.1 broadcast_in_dim.92
  58.4 0.1 broadcast_in_dim.91
  58.5 1.2 fusion.60
  59.9 0.1 broadcast_in_dim.92
  60.0 0.1 broadcast_in_dim.91
  60.1 1.2 fusion.60
  61.5 0.1 broadcast_in_dim.92
  61.7 0.1 broadcast_in_dim.91
  61.8 1.2 fusion.60
  63.2 0.1 broadcast_in_dim.92
  63.3 0.1 broadcast_in_dim.91
  63.4 1.2 fusion.60
  64.8 0.1 broadcast_in_dim.92
  65.0 0.1 broadcast_in_dim.91
  65.1 1.2 fusion.60
  66.4 0.1 broadcast_in_dim.65
  66.6 0.8 fusion.21
  67.4 3.4 %all-to-all-start.1 = ((f32[8,8,256]{2,1,0:T(8,128)}), f32[8,8,256]{2,1,0:T(8,128)S(1)}, u32[]{:S(2)}, u32[]{:S(2)}) async-start(f32[8,8,256]{2,1,0:T(8,128)} %fusion.21), calls=%async_computation.1 | async-start | bytes 131072 | tf_op jit(solution)/shard_map/all_to_all | solution.py:72
  70.8 4.9 %all-to-all-done.1 = f32[8,8,256]{2,1,0:T(8,128)S(1)} async-done(((f32[8,8,256]{2,1,0:T(8,128)}), f32[8,8,256]{2,1,0:T(8,128)S(1)}, u32[]{:S(2)}, u32[]{:S(2)}) %all-to-all-start.1) | async-done | bytes 65568 | tf_op jit(solution)/shard_map/all_to_all | solution.py:72
  75.7 0.1 fusion.33
  75.9 0.3 fusion.46
  76.3 0.2 select_reduce_fusion.1
  76.5 0.6 subtract_reduce_fusion
  77.1 0.4 multiply_reduce_fusion
  77.6 8.3 %all_gather.30 = bf16[64,2048]{1,0:T(8,128)(2,1)S(1)} all-gather(bf16[8,2048]{1,0:T(8,128)(2,1)S(1)} %subtract_convert_fusion), channel_id=1, replica_groups=mesh['grp'=4,'seq'=8] {'seq'}, dimensions={0}, use_global_device_ids=true | all-gather | bytes 294912 | tf_op jit(solution)/shard_map/all_gather | solution.py:89
  85.9 0.3 convolution_convert_fusion.2
  86.3 9.0 %all_gather.31 = bf16[64,1024]{1,0:T(8,128)(2,1)S(1)} all-gather(bf16[64,128]{1,0:T(8,128)(2,1)S(1)} %convolution_convert_fusion.2), channel_id=1, replica_groups=mesh['grp'=4,'seq'=8] {'seq'}, dimensions={1}, use_global_device_ids=true | all-gather | bytes 147456 | tf_op jit(solution)/shard_map/all_gather | solution.py:96
  95.3 1.1 convolution_convert_fusion
  96.6 0.1 reduce_sum.78
  96.8 0.3 fusion.5
  97.1 0.3 fusion.3
  97.4 0.8 copy.56
  98.2 0.2 fusion.7
  98.4 0.7 copy.98
  99.1 0.4 convolution_convert_fusion.1
  99.5 0.8 copy.57
  100.4 34.9 %all-reduce.3.cloned.1.call-done = bf16[128,2048]{1,0:T(8,128)(2,1)} async-done(((bf16[128,2048]{1,0:T(8,128)(2,1)}), bf16[128,2048]{1,0:T(8,128)(2,1)}) %all-reduce.3.cloned.1.call-update) | async-done | bytes 524304 | tf_op jit(solution)/shard_map/psum | solution.py:133
  135.2 1.9 %fusion.8 = f32[]{:T(128)} fusion(bf16[128,2048]{1,0:T(8,128)(2,1)} %all-reduce.3.cloned.1.call-done), kind=kLoop, calls=%fused_computation.25 | loop fusion | flops 786431 | bytes 524292 | tf_op jit(solution)/shard_map/reduce_sum | solution.py:134
  137.1 13.3 %all-reduce = (f32[1]{0:T(128)}, f32[]{:T(128)}) all-reduce(f32[1]{0:T(128)} %bitcast.19, f32[]{:T(128)} %fusion.8), channel_id=1, replica_groups=mesh['grp'=4,'seq'=8] {'seq'}, use_global_device_ids=true, to_apply=%region_9.10 | all-reduce | flops 2 | bytes 16 | tf_op jit(solution)/shard_map/psum | solution.py:134
  151.2 2.1 %convert_multiply_fusion = f32[128,2048]{1,0:T(8,128)} fusion(bf16[128,2048]{1,0:T(8,128)(2,1)} %all-reduce.3.cloned.1.call-done, f32[]{:T(128)S(6)} %rsqrt.15), kind=kLoop, calls=%fused_computation.11 | loop fusion | flops 524288 | bytes 1572868 | tf_op jit(solution)/shard_map/mul | solution.py:135
  153.3 18.9 %reduce-scatter.2.cloned.1.call-done = bf16[8,1024]{1,0:T(8,128)(2,1)} async-done(((bf16[64,1024]{1,0:T(8,128)(2,1)}), bf16[8,1024]{1,0:T(8,128)(2,1)}) %reduce-scatter.2.cloned.1.call-update) | async-done | bytes 16400 | tf_op jit(solution)/shard_map/reduce_scatter | solution.py:124
  (49 shorter events, 1.8 us)
Async XLA Ops:
  7.2 68.7 %copy-start = (bf16[2048,128]{1,0:T(8,128)(2,1)S(1)}, bf16[2048,128]{1,0:T(8,128)(2,1)}, u32[]{:S(2)}) copy-start(bf16[2048,128]{1,0:T(8,128)(2,1)} %param.17) | copy-start | bytes 1572868
  7.2 46.6 %all-gather.7.cloned.1.call-start = ((), (), s32[]{:S(2)}) async-start(), calls=%async_computation.3 | async-start | bytes 2359296 | tf_op jit(solution)/shard_map/all_gather | solution.py:13
  18.2 4.4 %copy-start.1 = (bf16[128,2048]{1,0:T(8,128)(2,1)S(1)}, bf16[128,2048]{1,0:T(8,128)(2,1)}, u32[]{:S(2)}) copy-start(bf16[128,2048]{1,0:T(8,128)(2,1)} %param.15) | copy-start | bytes 1572868
  23.5 43.1 %all-to-all-start = ((bf16[128,8,256]{2,0,1:T(8,128)(2,1)}), bf16[128,8,256]{2,0,1:T(8,128)(2,1)S(1)}, u32[]{:S(2)}, u32[]{:S(2)}) async-start(bf16[128,8,256]{2,0,1:T(8,128)(2,1)} %bitcast.109), calls=%async_computation | async-start | bytes 1048576 | tf_op jit(solution)/shard_map/all_to_all | solution.py:70
  54.7 21.2 %copy-start.2 = (f32[2048]{0:T(1024)S(1)}, f32[2048]{0:T(1024)}, u32[]{:S(2)}) copy-start(f32[2048]{0:T(1024)} %param.16) | copy-start | bytes 24580
  66.3 10.0 %copy-start.3 = (s32[1,8]{1,0:T(1,128)S(1)}, s32[1,8]{1,0:T(1,128)}, u32[]{:S(2)}) copy-start(s32[1,8]{1,0:T(1,128)} %param.14) | copy-start | bytes 100
  67.4 8.3 %all-to-all-start.1 = ((f32[8,8,256]{2,1,0:T(8,128)}), f32[8,8,256]{2,1,0:T(8,128)S(1)}, u32[]{:S(2)}, u32[]{:S(2)}) async-start(f32[8,8,256]{2,1,0:T(8,128)} %fusion.21), calls=%async_computation.1 | async-start | bytes 131072 | tf_op jit(solution)/shard_map/all_to_all | solution.py:72
  70.8 64.4 %all-reduce.3.cloned.1.call-start = ((), (), s32[]{:S(2)}) async-start(), calls=%async_computation.5 | async-start | bytes 1048576 | tf_op jit(solution)/shard_map/psum | solution.py:133
  96.4 75.8 %reduce-scatter.2.cloned.1.call-start = ((), (), s32[]{:S(2)}) async-start(), calls=%async_computation.4 | async-start | bytes 147456 | tf_op jit(solution)/shard_map/reduce_scatter | solution.py:124
Sparse Core Ops, SparseCore 0:
  22.8 30.9 all-gather.6
  96.5 38.6 all-reduce.2
  138.8 33.3 reduce-scatter.1
where the time goes:
time: 180 us; the launch traced here: 179 us
  blocking collectives  65.4 us (36%)
  waiting for transfers between devices  61.5 us (34%)
  other arithmetic  14.7 us (8%)
  between operations  14.7 us (8%)
  local copies, waits for them, and re-layouts  10.4 us (6%)
  starting transfers between devices  6.97 us (4%)
  matrix products  4.78 us (3%)
    psum x1, waiting for transfers between devices, body(): lax.psum(weight_part.astype(jnp.bfloat16), 'grp').astype(jnp.float32)  34.9 us
    all_gather x2, blocking collectives, joined(): gathered = jax.tree.map(lambda a: lax.all_gather(a, axis), part)  23.7 us
    reduce_scatter x1, waiting for transfers between devices, body(): lax.psum_scatter((terms.reshape(lax.axis_size('seq') * own_rows, channels...  18.9 us
    psum x1, blocking collectives, body(): lax.psum((local_loss, jnp.sum(weight_sum * weight_sum)), 'seq')  13.3 us
    all_gather x1, blocking collectives, body(): queries = lax.all_gather(latent_queries[0], 'seq', axis=0, tiled=True)  11 us
    all_gather x1, blocking collectives, body(): grad_attn = lax.all_gather(grad_cols, 'seq', axis=1, tiled=True)  9.03 us
    all_gather x1, blocking collectives, body(): grad_all = lax.all_gather(grad_hidden, 'seq', axis=0, tiled=True)  8.34 us
    add x7, other arithmetic, combine(): earlier[2] * repeat_heads(factor_one) + later[2] * repeat_heads(factor_two)  8.21 us
  transfers between devices with their start and end apart: 5, of which 4 were waited for; matrix products, arithmetic and copies ran while one was open for 12% of the time, Pallas kernels for 0%

commit v1 on v0

--- a/solution.py
+++ b/solution.py
@@ -1,3 +1,4 @@
+import functools
 import jax
 import jax.numpy as jnp
 from jax import lax
@@ -7,6 +8,13 @@
 HD = 128
 epsilon = 1e-06
 loss_factor = 64.0
+
+
+def begin_block_all(piece_in, mesh_ax):
+    return lax.all_gather(piece_in, mesh_ax).sum(axis=0)
+
+
+refer_the_cards = functools.partial(begin_block_all, mesh_ax="grp")
 
 
 def joined(part, axis, combine):
@@ -130,7 +138,7 @@
         tiled=True,
     )
     entries = channels * D
-    weight_sum = lax.psum(weight_part.astype(jnp.bfloat16), "grp").astype(jnp.float32)
+    weight_sum = refer_the_cards(weight_part.astype(jnp.bfloat16)).astype(jnp.float32)
     loss_sum, square_sum = lax.psum((local_loss, jnp.sum(weight_sum * weight_sum)), "seq")
     proj_update = weight_sum * lax.rsqrt(square_sum / entries + epsilon)
     return (

time: 180 us -> 176 us (0.978)
  waiting for transfers between devices: 61.5 us -> 57.5 us
    psum x1 -> x0, waiting for transfers between devices: 34.9 us -> none  [body(): lax.psum(weight_part.astype(jnp.bfloat16), 'grp').astype(jnp.float32)]
    all_gather x0 -> x1, waiting for transfers between devices: none -> 32.5 us  [begin_block_all(): return lax.all_gather(piece_in, mesh_ax).sum(axis=0)]
    reduce_sum x0 -> x1, other arithmetic: none -> 2.02 us  [begin_block_all(): return lax.all_gather(piece_in, mesh_ax).sum(axis=0)]
where the time goes in v1:
time: 176 us; the launch traced here: 175 us
  blocking collectives  66.2 us (38%)
  waiting for transfers between devices  57.5 us (33%)
  between operations  14.7 us (8%)
  other arithmetic  14.6 us (8%)
  local copies, waits for them, and re-layouts  10.4 us (6%)
  starting transfers between devices  6.97 us (4%)
  matrix products  4.77 us (3%)
    all_gather x1, waiting for transfers between devices, begin_block_all(): return lax.all_gather(piece_in, mesh_ax).sum(axis=0)  32.5 us
    all_gather x2, blocking collectives, joined(): gathered = jax.tree.map(lambda a: lax.all_gather(a, axis), part)  23.7 us
    reduce_scatter x1, waiting for transfers between devices, body(): lax.psum_scatter((terms.reshape(lax.axis_size('seq') * own_rows, channels...  17.3 us
    psum x1, blocking collectives, body(): lax.psum((local_loss, jnp.sum(weight_sum * weight_sum)), 'seq')  14.1 us
    all_gather x1, blocking collectives, body(): queries = lax.all_gather(latent_queries[0], 'seq', axis=0, tiled=True)  11 us
    all_gather x1, blocking collectives, body(): grad_attn = lax.all_gather(grad_cols, 'seq', axis=1, tiled=True)  9.03 us
    all_gather x1, blocking collectives, body(): grad_all = lax.all_gather(grad_hidden, 'seq', axis=0, tiled=True)  8.34 us
    add x7, other arithmetic, combine(): earlier[2] * repeat_heads(factor_one) + later[2] * repeat_heads(factor_two)  8.21 us
  transfers between devices with their start and end apart: 5, of which 4 were waited for; matrix products, arithmetic and copies ran while one was open for 12% of the time, Pallas kernels for 0%

profile of v1, /device:TPU:0, one launch (start us, length us, event | category | flops | bytes accessed | tf_op | source)
XLA Modules:
  0.0 175.4 jit_solution(5640138102276530314)
XLA Ops:
  7.2 11.0 %all-gather = bf16[1,64,1024]{2,1,0:T(8,128)(2,1)S(1)} all-gather(bf16[1,8,1024]{2,1,0:T(8,128)(2,1)} %param.12), channel_id=2, replica_groups=mesh['grp'=4,'seq'=8] {'seq'}, dimensions={1}, use_global_device_ids=true | all-gather | bytes 147456 | tf_op jit(solution)/shard_map/all_gather | solution.py:53
  18.3 1.0 copy.64
  19.3 1.0 copy.65
  20.3 0.7 broadcast_compare_fusion
  21.1 0.4 select_reduce_fusion
  21.4 0.3 convolution_bitcast_fusion
  21.7 0.2 copy.46
  21.9 0.7 all_gather_reshape.3
  22.6 0.8 copy.97
  23.5 3.5 %all-to-all-start = ((bf16[128,8,256]{2,0,1:T(8,128)(2,1)}), bf16[128,8,256]{2,0,1:T(8,128)(2,1)S(1)}, u32[]{:S(2)}, u32[]{:S(2)}) async-start(bf16[128,8,256]{2,0,1:T(8,128)(2,1)} %bitcast.110), calls=%async_computation | async-start | bytes 1048576 | tf_op jit(solution)/shard_map/all_to_all | solution.py:78
  27.0 0.3 fusion.15
  27.3 14.3 %all-gather.5 = f32[8,64,8]{1,2,0:T(8,128)S(1)} all-gather(f32[1,64,8]{1,2,0:T(8,128)S(1)} %bitcast.148), channel_id=4, replica_groups=mesh['grp'=4,'seq'=8] {'seq'}, dimensions={0}, use_global_device_ids=true | all-gather | bytes 18432 | tf_op jit(solution)/shard_map/all_gather | solution.py:21
  41.5 9.5 %all-gather.4 = f32[8,64,8]{1,2,0:T(8,128)S(1)} all-gather(f32[1,64,8]{1,2,0:T(8,128)S(1)} %bitcast.147), channel_id=3, replica_groups=mesh['grp'=4,'seq'=8] {'seq'}, dimensions={0}, use_global_device_ids=true | all-gather | bytes 18432 | tf_op jit(solution)/shard_map/all_gather | solution.py:21
  51.0 2.8 %all-gather.9.cloned.1.call-done = f32[8,64,1024]{2,1,0:T(8,128)} async-done(((f32[1,64,1024]{2,1,0:T(8,128)}), f32[8,64,1024]{2,1,0:T(8,128)}) %all-gather.9.cloned.1.call-update) | async-done | bytes 2097168 | tf_op jit(solution)/shard_map/all_gather | solution.py:21
  53.8 1.0 slice_bitcast_fusion
  54.7 11.5 %while.19 = (s32[]{:T(128)}, f32[64,8]{0,1:T(8,128)S(1)}, f32[64,8]{0,1:T(8,128)S(1)}, f32[64,1024]{1,0:T(8,128)S(1)}, f32[8,64,8]{1,2,0:T(8,128)S(1)}, /*index=...) while((s32[]{:T(128)}, f32[64,8]{0,1:T(8,128)S(1)}, ...), condition=%wide.region_3.4_spmd, body=%wide.region_2.3_spmd.sunk | while | flops 199685 | bytes 1863823 | solution.py:26
  54.9 0.1 broadcast_in_dim.92
  55.1 0.1 broadcast_in_dim.91
  55.2 1.2 fusion.60
  56.6 0.1 broadcast_in_dim.92
  56.7 0.1 broadcast_in_dim.91
  56.9 1.2 fusion.60
  58.2 0.1 broadcast_in_dim.92
  58.4 0.1 broadcast_in_dim.91
  58.5 1.2 fusion.60
  59.9 0.1 broadcast_in_dim.92
  60.0 0.1 broadcast_in_dim.91
  60.1 1.2 fusion.60
  61.5 0.1 broadcast_in_dim.92
  61.7 0.1 broadcast_in_dim.91
  61.8 1.2 fusion.60
  63.2 0.1 broadcast_in_dim.92
  63.3 0.1 broadcast_in_dim.91
  63.4 1.2 fusion.60
  64.8 0.1 broadcast_in_dim.92
  65.0 0.1 broadcast_in_dim.91
  65.1 1.2 fusion.60
  66.4 0.1 broadcast_in_dim.65
  66.6 0.8 fusion.21
  67.4 3.4 %all-to-all-start.1 = ((f32[8,8,256]{2,1,0:T(8,128)}), f32[8,8,256]{2,1,0:T(8,128)S(1)}, u32[]{:S(2)}, u32[]{:S(2)}) async-start(f32[8,8,256]{2,1,0:T(8,128)} %fusion.21), calls=%async_computation.1 | async-start | bytes 131072 | tf_op jit(solution)/shard_map/all_to_all | solution.py:80
  70.8 4.9 %all-to-all-done.1 = f32[8,8,256]{2,1,0:T(8,128)S(1)} async-done(((f32[8,8,256]{2,1,0:T(8,128)}), f32[8,8,256]{2,1,0:T(8,128)S(1)}, u32[]{:S(2)}, u32[]{:S(2)}) %all-to-all-start.1) | async-done | bytes 65568 | tf_op jit(solution)/shard_map/all_to_all | solution.py:80
  75.7 0.1 fusion.33
  75.9 0.3 fusion.46
  76.3 0.2 select_reduce_fusion.1
  76.5 0.6 subtract_reduce_fusion
  77.1 0.4 multiply_reduce_fusion
  77.6 8.3 %all_gather.36 = bf16[64,2048]{1,0:T(8,128)(2,1)S(1)} all-gather(bf16[8,2048]{1,0:T(8,128)(2,1)S(1)} %subtract_convert_fusion), channel_id=1, replica_groups=mesh['grp'=4,'seq'=8] {'seq'}, dimensions={0}, use_global_device_ids=true | all-gather | bytes 294912 | tf_op jit(solution)/shard_map/all_gather | solution.py:97
  85.9 1.1 convolution_convert_fusion
  87.1 0.3 convolution_convert_fusion.2
  87.4 9.0 %all_gather.37 = bf16[64,1024]{1,0:T(8,128)(2,1)S(1)} all-gather(bf16[64,128]{1,0:T(8,128)(2,1)S(1)} %convolution_convert_fusion.2), channel_id=1, replica_groups=mesh['grp'=4,'seq'=8] {'seq'}, dimensions={1}, use_global_device_ids=true | all-gather | bytes 147456 | tf_op jit(solution)/shard_map/all_gather | solution.py:104
  96.6 0.1 reduce_sum.90
  96.8 0.3 fusion.5
  97.1 0.3 fusion.3
  97.4 0.8 copy.56
  98.2 0.2 fusion.7
  98.4 0.7 copy.98
  99.1 0.4 convolution_convert_fusion.1
  99.5 0.8 copy.57
  100.4 32.5 %all-gather.11.cloned.1.call-done = bf16[512,2048]{1,0:T(8,128)(2,1)} async-done(((bf16[128,2048]{1,0:T(8,128)(2,1)}), bf16[512,2048]{1,0:T(8,128)(2,1)}) %all-gather.11.cloned.1.call-update) | async-done | bytes 2097168 | tf_op jit(solution)/shard_map/all_gather | solution.py:14
  132.9 2.0 %reduce_sum.91 = bf16[128,2048]{1,0:T(8,128)(2,1)S(1)} reduce(bf16[4,128,2048]{2,1,0:T(8,128)(2,1)} %bitcast.126, bf16[]{:T(256)} %constant.86.clone.1), dimensions={0}, to_apply=%region_13.14 | reduce | flops 786432 | bytes 2621442 | tf_op jit(solution)/shard_map/reduce_sum | solution.py:14
  134.9 0.9 fusion.8
  135.8 14.1 %all-reduce = (f32[1]{0:T(128)}, f32[]{:T(128)}) all-reduce(f32[1]{0:T(128)} %bitcast.19, f32[]{:T(128)} %fusion.8), channel_id=1, replica_groups=mesh['grp'=4,'seq'=8] {'seq'}, use_global_device_ids=true, to_apply=%region_9.10 | all-reduce | flops 2 | bytes 16 | tf_op jit(solution)/shard_map/psum | solution.py:142
  150.5 1.1 convert_multiply_fusion
  151.6 17.3 %reduce-scatter.2.cloned.1.call-done = bf16[8,1024]{1,0:T(8,128)(2,1)} async-done(((bf16[64,1024]{1,0:T(8,128)(2,1)}), bf16[8,1024]{1,0:T(8,128)(2,1)}) %reduce-scatter.2.cloned.1.call-update) | async-done | bytes 16400 | tf_op jit(solution)/shard_map/reduce_scatter | solution.py:132
  (50 shorter events, 1.9 us)
Async XLA Ops:
  7.2 68.7 %copy-start = (bf16[2048,128]{1,0:T(8,128)(2,1)S(1)}, bf16[2048,128]{1,0:T(8,128)(2,1)}, u32[]{:S(2)}) copy-start(bf16[2048,128]{1,0:T(8,128)(2,1)} %param.17) | copy-start | bytes 1572868
  7.2 46.6 %all-gather.9.cloned.1.call-start = ((), (), s32[]{:S(2)}) async-start(), calls=%async_computation.3 | async-start | bytes 2359296 | tf_op jit(solution)/shard_map/all_gather | solution.py:21
  18.2 4.4 %copy-start.1 = (bf16[128,2048]{1,0:T(8,128)(2,1)S(1)}, bf16[128,2048]{1,0:T(8,128)(2,1)}, u32[]{:S(2)}) copy-start(bf16[128,2048]{1,0:T(8,128)(2,1)} %param.15) | copy-start | bytes 1572868
  23.5 43.1 %all-to-all-start = ((bf16[128,8,256]{2,0,1:T(8,128)(2,1)}), bf16[128,8,256]{2,0,1:T(8,128)(2,1)S(1)}, u32[]{:S(2)}, u32[]{:S(2)}) async-start(bf16[128,8,256]{2,0,1:T(8,128)(2,1)} %bitcast.110), calls=%async_computation | async-start | bytes 1048576 | tf_op jit(solution)/shard_map/all_to_all | solution.py:78
  54.7 21.2 %copy-start.2 = (f32[2048]{0:T(1024)S(1)}, f32[2048]{0:T(1024)}, u32[]{:S(2)}) copy-start(f32[2048]{0:T(1024)} %param.16) | copy-start | bytes 24580
  66.3 10.0 %copy-start.3 = (s32[1,8]{1,0:T(1,128)S(1)}, s32[1,8]{1,0:T(1,128)}, u32[]{:S(2)}) copy-start(s32[1,8]{1,0:T(1,128)} %param.14) | copy-start | bytes 100
  67.4 8.3 %all-to-all-start.1 = ((f32[8,8,256]{2,1,0:T(8,128)}), f32[8,8,256]{2,1,0:T(8,128)S(1)}, u32[]{:S(2)}, u32[]{:S(2)}) async-start(f32[8,8,256]{2,1,0:T(8,128)} %fusion.21), calls=%async_computation.1 | async-start | bytes 131072 | tf_op jit(solution)/shard_map/all_to_all | solution.py:80
  70.8 62.1 %all-gather.11.cloned.1.call-start = ((), (), s32[]{:S(2)}) async-start(), calls=%async_computation.5 | async-start | bytes 2621440 | tf_op jit(solution)/shard_map/all_gather | solution.py:14
  87.1 81.8 %reduce-scatter.2.cloned.1.call-start = ((), (), s32[]{:S(2)}) async-start(), calls=%async_computation.4 | async-start | bytes 147456 | tf_op jit(solution)/shard_map/reduce_scatter | solution.py:132
Sparse Core Ops, SparseCore 0:
  22.8 30.9 all-gather.8
  87.2 45.6 all-gather.10
  136.5 32.3 reduce-scatter.1
